TPU v7x, 32 devices: a whole 2x2x4 slice. The times are simulated.
32 devices in a mesh: seq: 16 (over z, y, core), exp: 2 (over x).
Axes of the slice: x: 2, y: 2, z: 4, core: 2. Of those that a mesh axis runs over, the one named last changes fastest.
Arguments:
- hidden_in: bfloat16 [6, 6144], P('exp', 'seq'), may hold values from -2 to 2
- queries: bfloat16 [6, 6144], P(None, 'exp'), may hold values from -40 to 40
- key_cache: bfloat16 [6, 8192, 1024], P(None, 'seq', 'exp'), may hold values from -16 to 16
- value_cache: bfloat16 [6, 8192, 1024], P(None, 'seq', 'exp'), may hold values from -6 to 6
- lengths: int32 [6], replicated, may hold values from 2 to 8192
- out_weight: bfloat16 [6144, 6144], P('exp', 'seq'), may hold values from -0.078125 to 0.078125
- norm_gain: float32 [6144], P('seq'), may hold values from 0.1 to 1.9
- router: bfloat16 [6144, 8], P('seq'), may hold values from -0.078125 to 0.078125
- expert_ids: int32 [6, 2], P('exp'), may hold values from 0 to 7, as said below
- capacity: int32 [8], replicated, may hold values from 1 to 3, as said below
- w_gate: bfloat16 [8, 6144, 8192], P('exp', None, 'seq'), may hold values from -0.078125 to 0.078125
- w_up: bfloat16 [8, 6144, 8192], P('exp', None, 'seq'), may hold values from -0.078125 to 0.078125
- w_down: bfloat16 [8, 8192, 6144], P('exp', 'seq'), may hold values from -0.09375 to 0.09375
Outputs:
- layer_out: bfloat16 [6, 6144], P('exp', 'seq')
Inputs may be any that keep to these rules, and one draw needn't show every extreme that they name: lengths[b] counts sequence b's live cache positions, the newest token's included. `expert_ids`: the two experts of a token differ. One expert is named by every token; any other expert is named at most 3 times within one aligned block of 3 tokens. The expert that every token names has capacity 3.
All inputs are finite; a program needn't handle non-finite values.
Results may differ from a plain program's by a relative error of at most 0.0085.
Values may be sent and summed in bfloat16 or wider, within the bound.
A program may use at most 128 MiB of HBM per device.

v0:
```python
import math
import jax
import jax.numpy as jnp
from jax import lax
from jax.sharding import PartitionSpec as P

D = 6144
HEADS = 48
KV_HEADS = 8
HEAD_DIM = 128
EXPERTS = 8
masked_score = -1e30
norm_eps = 1e-05


def joined(value, axis, join):
    pieces = jax.tree.map(lambda part: lax.all_gather(part, axis), value)
    head = jax.tree.map(lambda part: part[0], pieces)
    tail = jax.tree.map(lambda part: part[1:], pieces)
    running, _ = lax.scan(lambda running, share: (join(running, share), None), head, tail)
    return running


def merge_partial_results(left_part, right_part):
    left_maximum_score, left_denom, left_sum = left_part
    right_peak, right_denom, right_sum = right_part
    joint_peak = jnp.maximum(left_maximum_score, right_peak)
    left_factor = jnp.exp(left_maximum_score - joint_peak)
    right_factor = jnp.exp(right_peak - joint_peak)
    return (
        joint_peak,
        left_denom * left_factor + right_denom * right_factor,
        left_sum * left_factor[..., None] + right_sum * right_factor[..., None],
    )


def on_device(
    hidden_in,
    queries,
    key_cache,
    value_cache,
    lengths,
    out_weight,
    norm_gain,
    router,
    expert_ids,
    capacity,
    w_gate,
    w_up,
    w_down,
):
    seq_count = queries.shape[0]
    group_size = HEADS // KV_HEADS
    kv_local = key_cache.shape[2] // HEAD_DIM
    span_local = key_cache.shape[1]
    query_heads = queries.reshape(seq_count, kv_local, group_size, HEAD_DIM)
    key_rows = key_cache.reshape(seq_count, span_local, kv_local, HEAD_DIM)
    value_rows = value_cache.reshape(seq_count, span_local, kv_local, HEAD_DIM).astype(jnp.float32)
    first_place = lax.axis_index("seq") * span_local
    places = first_place + jnp.arange(span_local, dtype=jnp.int32)
    live_mask = (places[None, :] < lengths[:, None])[:, None, None, :]
    scores = jnp.einsum(
        "bkgd,bjkd->bkgj", query_heads, key_rows, preferred_element_type=jnp.float32
    ) * (1.0 / math.sqrt(HEAD_DIM))
    scores = jnp.where(live_mask, scores, masked_score)
    local_peak = jnp.max(scores, axis=-1)
    attn_weights = jnp.where(live_mask, jnp.exp(scores - local_peak[..., None]), 0.0)
    local_sum = jnp.einsum(
        "bkgj,bjkd->bkgd", attn_weights, value_rows, precision=lax.Precision.HIGHEST
    )
    global_peak, denom_sum, weighted = joined(
        (local_peak, jnp.sum(attn_weights, axis=-1), local_sum), "seq", merge_partial_results
    )
    attended = (
        (weighted / denom_sum[..., None])
        .reshape(seq_count, kv_local * group_size * HEAD_DIM)
        .astype(jnp.bfloat16)
    )
    partial_value = jnp.dot(attended, out_weight, preferred_element_type=jnp.float32)
    projected = lax.psum_scatter(partial_value, "exp", scatter_dimension=0, tiled=True)
    residual = hidden_in.astype(jnp.float32) + projected
    gained = residual * norm_gain
    router_wide = router.astype(jnp.float32)
    squares = jnp.sum(residual * residual, axis=-1)
    total_sq = lax.psum(squares, "seq")
    scale_row = lax.rsqrt(total_sq / D + norm_eps)
    logits = lax.psum(
        jnp.dot(gained * scale_row[:, None], router_wide, precision=lax.Precision.HIGHEST), "seq"
    )
    normed = (gained * scale_row[:, None]).astype(jnp.bfloat16)
    row_total = expert_ids.shape[0]
    onehot_int = (
        expert_ids[:, :, None] == jnp.arange(EXPERTS, dtype=jnp.int32)[None, None, :]
    ).astype(jnp.int32)
    name_count = jnp.sum(onehot_int, axis=1)
    row_order = jnp.arange(row_total, dtype=jnp.int32)
    before = (row_order[None, :] < row_order[:, None]).astype(jnp.int32)
    earlier = jnp.dot(before, name_count)
    slot_rank = jnp.sum(onehot_int * earlier[:, None, :], axis=-1)
    slot_limit = jnp.sum(onehot_int * capacity[None, None, :], axis=-1)
    kept_mask = (slot_rank < slot_limit).astype(jnp.float32)
    expert_indicator = onehot_int.astype(jnp.float32)
    chosen = jnp.sum(expert_indicator * logits[:, None, :], axis=-1)
    gate_weight = jax.nn.sigmoid(chosen - chosen[:, ::-1])
    slot_match = (slot_rank[:, :, None] == row_order[None, None, :]).astype(jnp.float32)
    placing = jnp.einsum("rke,rks->esr", expert_indicator * kept_mask[:, :, None], slot_match)
    buffer = jnp.einsum(
        "esr,rd->esd", placing.astype(jnp.bfloat16), normed, preferred_element_type=jnp.float32
    ).astype(jnp.bfloat16)
    dispatched = lax.all_to_all(buffer, "exp", split_axis=0, concat_axis=1, tiled=True)
    shard_rows = lax.all_gather(dispatched, "seq", axis=2, tiled=True)
    gate_next = jnp.einsum("ern,enf->erf", shard_rows, w_gate, preferred_element_type=jnp.float32)
    up_next = jnp.einsum("ern,enf->erf", shard_rows, w_up, preferred_element_type=jnp.float32)
    hidden_act = (jax.nn.silu(gate_next) * up_next).astype(jnp.bfloat16)
    partial_out = jnp.einsum("erf,efd->erd", hidden_act, w_down, preferred_element_type=jnp.float32)
    blend_table = jnp.einsum(
        "rke,rks->esr", expert_indicator * (gate_weight * kept_mask)[:, :, None], slot_match
    )
    reduced_output = lax.psum_scatter(partial_out, "seq", scatter_dimension=2, tiled=True)
    returned = lax.all_to_all(reduced_output, "exp", split_axis=1, concat_axis=0, tiled=True)
    combined = jnp.einsum("esr,esd->rd", blend_table, returned, precision=lax.Precision.HIGHEST)
    return (residual + combined).astype(jnp.bfloat16)


def solution(mesh):
    in_specs = (
        P("exp", "seq"),
        P(None, "exp"),
        P(None, "seq", "exp"),
        P(None, "seq", "exp"),
        P(),
        P("exp", "seq"),
        P("seq"),
        P("seq", None),
        P("exp", None),
        P(),
        P("exp", None, "seq"),
        P("exp", None, "seq"),
        P("exp", "seq", None),
    )
    out_specs = P("exp", "seq")
    return jax.shard_map(
        on_device, mesh=mesh, in_specs=in_specs, out_specs=out_specs, check_vma=False
    )
```

profile of v0, /device:TPU:0, one launch (start us, length us, event | category | flops | bytes accessed | tf_op | source)
XLA Modules:
  0.0 272.3 jit_solution(8240845647066863271)
XLA Ops:
  6.5 1.6 reshape.56
  9.1 1.8 fusion.49
  10.9 1.4 fusion.4
  13.1 23.7 %all-gather = f32[96,4,6]{2,1,0:T(4,128)S(1)} all-gather(f32[6,4,6]{2,1,0:T(4,128)S(1)} %get-tuple-element.74), channel_id=2, replica_groups=mesh['seq'=16,'exp'=2] {'seq'}, dimensions={0}, use_global_device_ids=true | all-gather | bytes 9792 | tf_op jit(solution)/shard_map/all_gather | solution.py:17
  37.0 18.4 %all-gather.1 = f32[96,4,6]{2,1,0:T(4,128)S(1)} all-gather(f32[6,4,6]{2,1,0:T(4,128)S(1)} %fusion.20), channel_id=3, replica_groups=mesh['seq'=16,'exp'=2] {'seq'}, dimensions={0}, use_global_device_ids=true | all-gather | bytes 9792 | tf_op jit(solution)/shard_map/all_gather | solution.py:17
  57.9 2.3 slice.35
  60.3 16.4 %while.14 = (s32[]{:T(128)}, f32[6,4,6]{2,1,0:T(4,128)S(1)}, f32[6,4,6]{2,1,0:T(4,128)S(1)}, f32[6,4,6,128]{3,2,1,0:T(8,128)S(1)}, f32[15,6,4,6]{3,2,1,0:T(4,128...) while((s32[]{:T(128)}, f32[6,4,6]{2,1,0:T(4,128)S(1)}, ...), condition=%wide.region_3.4_spmd, body=%wide.region_2.3_spmd.sunk | while | flops 56162 | bytes 374501 | solution.py:20
  60.3 0.9 constant_dynamic-slice_fusion.2
  62.5 0.9 constant_dynamic-slice_fusion.2
  63.6 0.9 constant_dynamic-slice_fusion.2
  64.7 0.9 constant_dynamic-slice_fusion.2
  65.8 0.9 constant_dynamic-slice_fusion.2
  66.9 0.9 constant_dynamic-slice_fusion.2
  67.9 0.9 constant_dynamic-slice_fusion.2
  69.0 0.9 constant_dynamic-slice_fusion.2
  70.1 0.9 constant_dynamic-slice_fusion.2
  71.2 0.9 constant_dynamic-slice_fusion.2
  72.3 0.9 constant_dynamic-slice_fusion.2
  73.4 0.9 constant_dynamic-slice_fusion.2
  75.6 0.9 constant_dynamic-slice_fusion.2
  77.2 8.1 %all-reduce = f32[6,384]{1,0:T(8,128)S(1)} all-reduce(f32[6,384]{1,0:T(8,128)S(1)} %fusion.50), channel_id=5, replica_groups=mesh['seq'=16,'exp'=2] {'exp'}, use_global_device_ids=true, to_apply=%region_4.5.clone | all-reduce | flops 2304 | bytes 18432
  85.5 29.5 %psum.14 = f32[3]{0:T(128)S(1)} all-reduce(f32[3]{0:T(128)S(1)} %multiply_reduce_fusion), channel_id=1, replica_groups=mesh['seq'=16,'exp'=2] {'seq'}, use_global_device_ids=true, to_apply=%region_9.10 | all-reduce | flops 3 | bytes 24 | tf_op jit(solution)/shard_map/psum | solution.py:85
  115.5 29.5 %psum.15 = f32[3,8]{1,0:T(4,128)S(1)} all-reduce(f32[3,8]{1,0:T(4,128)S(1)} %fusion.26), channel_id=1, replica_groups=mesh['seq'=16,'exp'=2] {'seq'}, use_global_device_ids=true, to_apply=%region_10.11 | all-reduce | flops 24 | bytes 192 | tf_op jit(solution)/shard_map/psum | solution.py:87
  145.7 6.3 %all_to_all.36 = bf16[8,3,384]{2,1,0:T(4,128)(2,1)S(1)} all-to-all(bf16[8,3,384]{2,1,0:T(4,128)(2,1)S(1)} %copy.33), channel_id=1, replica_groups=mesh['seq'=16,'exp'=2] {'exp'}, dimensions={0} | all-to-all | bytes 36864 | tf_op jit(solution)/shard_map/all_to_all | solution.py:110
  152.0 18.3 %all_gather.27 = bf16[4,6,6144]{2,1,0:T(8,128)(2,1)S(1)} all-gather(bf16[4,6,384]{2,1,0:T(8,128)(2,1)S(1)} %copy.35), channel_id=1, replica_groups=mesh['seq'=16,'exp'=2] {'seq'}, dimensions={2}, use_global_device_ids=true | all-gather | bytes 313344 | tf_op jit(solution)/shard_map/all_gather | solution.py:111
  170.3 9.9 %fusion.51 = f32[4,6,512]{2,1,0:T(8,128)S(1)} fusion(bf16[4,6,6144]{2,1,0:T(8,128)(2,1)S(1)} %all_gather.27, bf16[4,6144,512]{2,1,0:T(8,128)(2,1)} %param.25), kind=kOutput, calls=%fused_computation.70 | convolution fusion | flops 150994944 | bytes 25509888 | tf_op jit(solution)/shard_map/ern,enf->erf/dot_general | solution.py:112
  180.2 9.9 %fusion.16 = bf16[4,6,512]{2,1,0:T(8,128)(2,1)S(1)} fusion(bf16[4,6,6144]{2,1,0:T(8,128)(2,1)S(1)} %all_gather.27, bf16[4,6144,512]{2,1,0:T(8,128)(2,1)} %param.26, f32[4,6,512]{2,1,0:T(8,128)S(1)} %fusion.51), kind=kOutput, calls=%fused_computation.19 | convolution fusion | flops 151068672 | bytes 25534464 | tf_op jit(solution)/shard_map/ern,enf->erf/dot_general | solution.py:113
  190.1 10.9 %fusion.52 = f32[4,6,6144]{2,1,0:T(8,128)} fusion(bf16[4,6,512]{2,1,0:T(8,128)(2,1)S(1)} %fusion.16, bf16[4,512,6144]{2,1,0:T(8,128)(2,1)} %param.27), kind=kOutput, calls=%fused_computation.71 | convolution fusion | flops 150994944 | bytes 25780224 | tf_op jit(solution)/shard_map/erf,efd->erd/dot_general | solution.py:115
  201.1 54.9 %reduce-scatter.2.cloned.1.call-done = f32[4,6,384]{2,1,0:T(8,128)} async-done(((f32[4,6,6144]{2,1,0:T(8,128)}), f32[4,6,384]{2,1,0:T(8,128)}) %reduce-scatter.2.cloned.1.call-update) | async-done | bytes 36880 | tf_op jit(solution)/shard_map/reduce_scatter | solution.py:119
  255.9 1.4 copy.36
  257.4 3.3 %all-to-all-start.1 = ((f32[4,6,384]{2,0,1:T(4,128)}), f32[4,6,384]{2,0,1:T(4,128)S(1)}, u32[]{:S(2)}, u32[]{:S(2)}) async-start(f32[4,6,384]{2,0,1:T(4,128)} %copy.36), calls=%async_computation.2 | async-start | bytes 73728 | tf_op jit(solution)/shard_map/all_to_all | solution.py:120
  260.9 3.7 %all-to-all-done.1 = f32[4,6,384]{2,0,1:T(4,128)S(1)} async-done(((f32[4,6,384]{2,0,1:T(4,128)}), f32[4,6,384]{2,0,1:T(4,128)S(1)}, u32[]{:S(2)}, u32[]{:S(2)}) %all-to-all-start.1) | async-done | bytes 36896 | tf_op jit(solution)/shard_map/all_to_all | solution.py:120
  (91 shorter events, 11.2 us)
Async XLA Ops:
  6.5 2.5 copy-start
  6.5 50.4 %all-gather.5.cloned.1.call-start = ((), (), s32[]{:S(2)}) async-start(), calls=%async_computation.4 | async-start | bytes 1253376 | tf_op jit(solution)/shard_map/all_gather | solution.py:17
  8.2 2.7 %copy-start.2 = (bf16[6,512,512]{2,1,0:T(8,128)(2,1)S(1)}, bf16[6,512,512]{2,1,0:T(8,128)(2,1)}, u32[]{:S(2)}) copy-start(bf16[6,512,512]{2,1,0:T(8,128)(2,1)} %param.18) | copy-start | bytes 9437188
  10.9 44.5 %copy-start.5 = (s32[3,2]{0,1:T(2,128)S(1)}, s32[3,2]{0,1:T(2,128)}, u32[]{:S(2)}) copy-start(s32[3,2]{0,1:T(2,128)} %param.23) | copy-start | bytes 76
  10.9 44.6 %copy-start.9 = (u32[32]{0:T(128)S(1)}, u32[32]{0:T(128)}, u32[]{:S(2)}) copy-start(u32[32]{0:T(128)} %constant.44) | copy-start | bytes 388
  13.0 242.9 %reduce-scatter.2.cloned.1.call-start = ((), (), s32[]{:S(2)}) async-start(), calls=%async_computation.3 | async-start | bytes 835584 | tf_op jit(solution)/shard_map/reduce_scatter | solution.py:119
  37.0 39.8 %copy-start.3 = (bf16[3072,384]{1,0:T(8,128)(2,1)S(1)}, bf16[3072,384]{1,0:T(8,128)(2,1)}, u32[]{:S(2)}) copy-start(bf16[3072,384]{1,0:T(8,128)(2,1)} %param.20) | copy-start | bytes 7077892
  60.2 25.0 %copy-start.4 = (bf16[3,384]{1,0:T(4,128)(2,1)S(1)}, bf16[3,384]{1,0:T(4,128)(2,1)}, u32[]{:S(2)}) copy-start(bf16[3,384]{1,0:T(4,128)(2,1)} %param.15) | copy-start | bytes 6916
  60.3 54.8 %copy-start.7 = (bf16[384,8]{0,1:T(8,128)(2,1)S(1)}, bf16[384,8]{0,1:T(8,128)(2,1)}, u32[]{:S(2)}) copy-start(bf16[384,8]{0,1:T(8,128)(2,1)} %param.22) | copy-start | bytes 18436
  60.3 54.8 %copy-start.8 = (f32[384]{0:T(512)S(1)}, f32[384]{0:T(512)}, u32[]{:S(2)}) copy-start(f32[384]{0:T(512)} %param.21) | copy-start | bytes 4612
  60.3 55.0 %copy-start.6 = (s32[8]{0:T(128)S(1)}, s32[8]{0:T(128)}, u32[]{:S(2)}) copy-start(s32[8]{0:T(128)} %param.24) | copy-start | bytes 100
  190.1 75.3 %copy-start.1 = (bf16[6,512,512]{2,1,0:T(8,128)(2,1)S(1)}, bf16[6,512,512]{2,1,0:T(8,128)(2,1)}, u32[]{:S(2)}) copy-start(bf16[6,512,512]{2,1,0:T(8,128)(2,1)} %param.17) | copy-start | bytes 9437188
  257.4 7.2 %all-to-all-start.1 = ((f32[4,6,384]{2,0,1:T(4,128)}), f32[4,6,384]{2,0,1:T(4,128)S(1)}, u32[]{:S(2)}, u32[]{:S(2)}) async-start(f32[4,6,384]{2,0,1:T(4,128)} %copy.36), calls=%async_computation.2 | async-start | bytes 73728 | tf_op jit(solution)/shard_map/all_to_all | solution.py:120
Sparse Core Ops, SparseCore 0:
  13.1 41.2 all-gather.4
  201.2 54.6 reduce-scatter.1
where the time goes:
time: 273 us; the launch traced here: 272 us
  blocking collectives  134 us (49%)
  waiting for transfers between devices  58.6 us (21%)
  matrix products  36.3 us (13%)
  local copies, waits for them, and re-layouts  21.4 us (8%)
  between operations  14.3 us (5%)
  other arithmetic  4.47 us (2%)
  starting transfers between devices  3.3 us (1%)
    reduce_scatter x1, waiting for transfers between devices, on_device(): lax.psum_scatter(partial_out, 'seq', scatter_dimension=2, tiled=True)  54.9 us
    all_gather x2, blocking collectives, joined(): pieces = jax.tree.map(lambda part: lax.all_gather(part, axis), value)  42.1 us
    psum x1, blocking collectives, on_device(): lax.psum(jnp.dot(gained * scale_row[:, None], router_wide, precision=lax....  29.5 us
    psum x1, blocking collectives, on_device(): total_sq = lax.psum(squares, 'seq')  29.5 us
    all_gather x1, blocking collectives, on_device(): shard_rows = lax.all_gather(dispatched, 'seq', axis=2, tiled=True)  18.3 us
    dynamic_slice x15, local copies, waits for them, and re-layouts, joined(): lax.scan(lambda running, share: (join(running, share), None), head, tail)  13.4 us
    dot_general x1, matrix products, on_device(): jnp.einsum('erf,efd->erd', hidden_act, w_down, preferred_element_type=jnp...  10.9 us
    dot_general x1, matrix products, on_device(): jnp.einsum('ern,enf->erf', shard_rows, w_up, preferred_element_type=jnp.f...  9.94 us
  transfers between devices with their start and end apart: 3, of which 2 were waited for; matrix products, arithmetic and copies ran while one was open for 1% of the time, Pallas kernels for 0%

commit v1 on v0

--- a/solution.py
+++ b/solution.py
@@ -84,8 +84,9 @@
     squares = jnp.sum(residual * residual, axis=-1)
     total_sq = lax.psum(squares, "seq")
     scale_row = lax.rsqrt(total_sq / D + norm_eps)
-    logits = lax.psum(
-        jnp.dot(gained * scale_row[:, None], router_wide, precision=lax.Precision.HIGHEST), "seq"
+    switch_region_now = lambda own_rows: lax.all_gather(own_rows, "seq").sum(axis=0)
+    logits = switch_region_now(
+        jnp.dot(gained * scale_row[:, None], router_wide, precision=lax.Precision.HIGHEST)
     )
     normed = (gained * scale_row[:, None]).astype(jnp.bfloat16)
     row_total = expert_ids.shape[0]

time: 273 us -> 261 us (0.956)
  blocking collectives: 134 us -> 123 us
    psum x1 -> x0, blocking collectives: 29.5 us -> none  [on_device(): lax.psum(jnp.dot(gained * scale_row[:, None], router_wide, precision=lax....]
    all_gather x0 -> x1, blocking collectives: none -> 17.2 us  [on_device(): lax.all_gather(own_rows, 'seq').sum(axis=0)]
where the time goes in v1:
time: 261 us; the launch traced here: 260 us
  blocking collectives  123 us (47%)
  waiting for transfers between devices  56.8 us (22%)
  matrix products  36.3 us (14%)
  local copies, waits for them, and re-layouts  21.4 us (8%)
  between operations  14.2 us (5%)
  other arithmetic  4.49 us (2%)
  starting transfers between devices  3.3 us (1%)
    reduce_scatter x1, waiting for transfers between devices, on_device(): lax.psum_scatter(partial_out, 'seq', scatter_dimension=2, tiled=True)  53 us
    all_gather x2, blocking collectives, joined(): pieces = jax.tree.map(lambda part: lax.all_gather(part, axis), value)  42.1 us
    psum x1, blocking collectives, on_device(): total_sq = lax.psum(squares, 'seq')  29.5 us
    all_gather x1, blocking collectives, on_device(): shard_rows = lax.all_gather(dispatched, 'seq', axis=2, tiled=True)  20.2 us
    all_gather x1, blocking collectives, on_device(): lax.all_gather(own_rows, 'seq').sum(axis=0)  17.2 us
    dynamic_slice x15, local copies, waits for them, and re-layouts, joined(): lax.scan(lambda running, share: (join(running, share), None), head, tail)  13.4 us
    dot_general x1, matrix products, on_device(): jnp.einsum('erf,efd->erd', hidden_act, w_down, preferred_element_type=jnp...  10.9 us
    dot_general x1, matrix products, on_device(): jnp.einsum('ern,enf->erf', shard_rows, w_up, preferred_element_type=jnp.f...  9.94 us
  transfers between devices with their start and end apart: 3, of which 2 were waited for; matrix products, arithmetic and copies ran while one was open for 1% of the time, Pallas kernels for 0%

profile of v1, /device:TPU:0, one launch (start us, length us, event | category | flops | bytes accessed | tf_op | source)
XLA Modules:
  0.0 260.1 jit_solution(2362982785176055378)
XLA Ops:
  6.5 1.6 reshape.56
  9.1 1.8 fusion.48
  10.9 1.4 fusion.4
  13.1 23.7 %all-gather = f32[96,4,6]{2,1,0:T(4,128)S(1)} all-gather(f32[6,4,6]{2,1,0:T(4,128)S(1)} %get-tuple-element.74), channel_id=2, replica_groups=mesh['seq'=16,'exp'=2] {'seq'}, dimensions={0}, use_global_device_ids=true | all-gather | bytes 9792 | tf_op jit(solution)/shard_map/all_gather | solution.py:17
  37.0 18.4 %all-gather.1 = f32[96,4,6]{2,1,0:T(4,128)S(1)} all-gather(f32[6,4,6]{2,1,0:T(4,128)S(1)} %fusion.20), channel_id=3, replica_groups=mesh['seq'=16,'exp'=2] {'seq'}, dimensions={0}, use_global_device_ids=true | all-gather | bytes 9792 | tf_op jit(solution)/shard_map/all_gather | solution.py:17
  58.0 2.3 slice.35
  60.4 16.4 %while.14 = (s32[]{:T(128)}, f32[6,4,6]{2,1,0:T(4,128)S(1)}, f32[6,4,6]{2,1,0:T(4,128)S(1)}, f32[6,4,6,128]{3,2,1,0:T(8,128)S(1)}, f32[15,6,4,6]{3,2,1,0:T(4,128...) while((s32[]{:T(128)}, f32[6,4,6]{2,1,0:T(4,128)S(1)}, ...), condition=%wide.region_3.4_spmd, body=%wide.region_2.3_spmd.sunk | while | flops 56162 | bytes 374501 | solution.py:20
  60.4 0.9 constant_dynamic-slice_fusion.2
  61.5 0.9 constant_dynamic-slice_fusion.2
  62.6 0.9 constant_dynamic-slice_fusion.2
  63.7 0.9 constant_dynamic-slice_fusion.2
  64.8 0.9 constant_dynamic-slice_fusion.2
  67.0 0.9 constant_dynamic-slice_fusion.2
  68.0 0.9 constant_dynamic-slice_fusion.2
  69.1 0.9 constant_dynamic-slice_fusion.2
  71.3 0.9 constant_dynamic-slice_fusion.2
  72.4 0.9 constant_dynamic-slice_fusion.2
  73.5 0.9 constant_dynamic-slice_fusion.2
  74.6 0.9 constant_dynamic-slice_fusion.2
  75.7 0.9 constant_dynamic-slice_fusion.2
  77.3 8.1 %all-reduce = f32[6,384]{1,0:T(8,128)S(1)} all-reduce(f32[6,384]{1,0:T(8,128)S(1)} %fusion.49), channel_id=6, replica_groups=mesh['seq'=16,'exp'=2] {'exp'}, use_global_device_ids=true, to_apply=%region_4.5.clone | all-reduce | flops 2304 | bytes 18432
  85.8 29.5 %psum.7 = f32[3]{0:T(128)S(1)} all-reduce(f32[3]{0:T(128)S(1)} %multiply_reduce_fusion), channel_id=1, replica_groups=mesh['seq'=16,'exp'=2] {'seq'}, use_global_device_ids=true, to_apply=%region_9.10 | all-reduce | flops 3 | bytes 24 | tf_op jit(solution)/shard_map/psum | solution.py:85
  115.5 17.2 %all-gather.4 = f32[16,3,8]{2,1,0:T(4,128)S(1)} all-gather(f32[1,3,8]{2,1,0:T(4,128)S(1)} %convolution_bitcast_fusion.2), channel_id=5, replica_groups=mesh['seq'=16,'exp'=2] {'seq'}, dimensions={0}, use_global_device_ids=true | all-gather | bytes 1632 | tf_op jit(solution)/shard_map/all_gather | solution.py:87
  133.5 6.3 %all_to_all.36 = bf16[8,3,384]{2,1,0:T(4,128)(2,1)S(1)} all-to-all(bf16[8,3,384]{2,1,0:T(4,128)(2,1)S(1)} %copy.33), channel_id=1, replica_groups=mesh['seq'=16,'exp'=2] {'exp'}, dimensions={0} | all-to-all | bytes 36864 | tf_op jit(solution)/shard_map/all_to_all | solution.py:111
  139.7 20.2 %all_gather.35 = bf16[4,6,6144]{2,1,0:T(8,128)(2,1)S(1)} all-gather(bf16[4,6,384]{2,1,0:T(8,128)(2,1)S(1)} %copy.35), channel_id=1, replica_groups=mesh['seq'=16,'exp'=2] {'seq'}, dimensions={2}, use_global_device_ids=true | all-gather | bytes 313344 | tf_op jit(solution)/shard_map/all_gather | solution.py:112
  159.9 9.9 %fusion.50 = f32[4,6,512]{2,1,0:T(8,128)S(1)} fusion(bf16[4,6,6144]{2,1,0:T(8,128)(2,1)S(1)} %all_gather.35, bf16[4,6144,512]{2,1,0:T(8,128)(2,1)} %param.25), kind=kOutput, calls=%fused_computation.70 | convolution fusion | flops 150994944 | bytes 25509888 | tf_op jit(solution)/shard_map/ern,enf->erf/dot_general | solution.py:113
  169.8 9.9 %fusion.16 = bf16[4,6,512]{2,1,0:T(8,128)(2,1)S(1)} fusion(bf16[4,6,6144]{2,1,0:T(8,128)(2,1)S(1)} %all_gather.35, bf16[4,6144,512]{2,1,0:T(8,128)(2,1)} %param.26, f32[4,6,512]{2,1,0:T(8,128)S(1)} %fusion.50), kind=kOutput, calls=%fused_computation.19 | convolution fusion | flops 151068672 | bytes 25534464 | tf_op jit(solution)/shard_map/ern,enf->erf/dot_general | solution.py:114
  179.7 10.9 %fusion.51 = f32[4,6,6144]{2,1,0:T(8,128)} fusion(bf16[4,6,512]{2,1,0:T(8,128)(2,1)S(1)} %fusion.16, bf16[4,512,6144]{2,1,0:T(8,128)(2,1)} %param.27), kind=kOutput, calls=%fused_computation.71 | convolution fusion | flops 150994944 | bytes 25780224 | tf_op jit(solution)/shard_map/erf,efd->erd/dot_general | solution.py:116
  190.7 53.0 %reduce-scatter.2.cloned.1.call-done = f32[4,6,384]{2,1,0:T(8,128)} async-done(((f32[4,6,6144]{2,1,0:T(8,128)}), f32[4,6,384]{2,1,0:T(8,128)}) %reduce-scatter.2.cloned.1.call-update) | async-done | bytes 36880 | tf_op jit(solution)/shard_map/reduce_scatter | solution.py:120
  243.7 1.4 copy.36
  245.2 3.3 %all-to-all-start.1 = ((f32[4,6,384]{2,0,1:T(4,128)}), f32[4,6,384]{2,0,1:T(4,128)S(1)}, u32[]{:S(2)}, u32[]{:S(2)}) async-start(f32[4,6,384]{2,0,1:T(4,128)} %copy.36), calls=%async_computation.2 | async-start | bytes 73728 | tf_op jit(solution)/shard_map/all_to_all | solution.py:121
  248.7 3.7 %all-to-all-done.1 = f32[4,6,384]{2,0,1:T(4,128)S(1)} async-done(((f32[4,6,384]{2,0,1:T(4,128)}), f32[4,6,384]{2,0,1:T(4,128)S(1)}, u32[]{:S(2)}, u32[]{:S(2)}) %all-to-all-start.1) | async-done | bytes 36896 | tf_op jit(solution)/shard_map/all_to_all | solution.py:121
  (92 shorter events, 11.2 us)
Async XLA Ops:
  6.5 2.5 copy-start
  6.5 50.6 %all-gather.7.cloned.1.call-start = ((), (), s32[]{:S(2)}) async-start(), calls=%async_computation.4 | async-start | bytes 1253376 | tf_op jit(solution)/shard_map/all_gather | solution.py:17
  8.2 2.7 %copy-start.2 = (bf16[6,512,512]{2,1,0:T(8,128)(2,1)S(1)}, bf16[6,512,512]{2,1,0:T(8,128)(2,1)}, u32[]{:S(2)}) copy-start(bf16[6,512,512]{2,1,0:T(8,128)(2,1)} %param.18) | copy-start | bytes 9437188
  10.9 44.5 %copy-start.5 = (s32[3,2]{0,1:T(2,128)S(1)}, s32[3,2]{0,1:T(2,128)}, u32[]{:S(2)}) copy-start(s32[3,2]{0,1:T(2,128)} %param.23) | copy-start | bytes 76
  10.9 44.6 %copy-start.9 = (u32[32]{0:T(128)S(1)}, u32[32]{0:T(128)}, u32[]{:S(2)}) copy-start(u32[32]{0:T(128)} %constant.44) | copy-start | bytes 388
  13.0 230.7 %reduce-scatter.2.cloned.1.call-start = ((), (), s32[]{:S(2)}) async-start(), calls=%async_computation.3 | async-start | bytes 835584 | tf_op jit(solution)/shard_map/reduce_scatter | solution.py:120
  37.0 39.9 %copy-start.3 = (bf16[3072,384]{1,0:T(8,128)(2,1)S(1)}, bf16[3072,384]{1,0:T(8,128)(2,1)}, u32[]{:S(2)}) copy-start(bf16[3072,384]{1,0:T(8,128)(2,1)} %param.20) | copy-start | bytes 7077892
  60.4 25.0 %copy-start.4 = (bf16[3,384]{1,0:T(4,128)(2,1)S(1)}, bf16[3,384]{1,0:T(4,128)(2,1)}, u32[]{:S(2)}) copy-start(bf16[3,384]{1,0:T(4,128)(2,1)} %param.15) | copy-start | bytes 6916
  60.4 25.1 %copy-start.6 = (s32[8]{0:T(128)S(1)}, s32[8]{0:T(128)}, u32[]{:S(2)}) copy-start(s32[8]{0:T(128)} %param.24) | copy-start | bytes 100
  60.4 54.9 %copy-start.7 = (bf16[384,8]{0,1:T(8,128)(2,1)S(1)}, bf16[384,8]{0,1:T(8,128)(2,1)}, u32[]{:S(2)}) copy-start(bf16[384,8]{0,1:T(8,128)(2,1)} %param.22) | copy-start | bytes 18436
  60.4 54.9 %copy-start.8 = (f32[384]{0:T(512)S(1)}, f32[384]{0:T(512)}, u32[]{:S(2)}) copy-start(f32[384]{0:T(512)} %param.21) | copy-start | bytes 4612
  179.7 73.5 %copy-start.1 = (bf16[6,512,512]{2,1,0:T(8,128)(2,1)S(1)}, bf16[6,512,512]{2,1,0:T(8,128)(2,1)}, u32[]{:S(2)}) copy-start(bf16[6,512,512]{2,1,0:T(8,128)(2,1)} %param.17) | copy-start | bytes 9437188
  245.2 7.2 %all-to-all-start.1 = ((f32[4,6,384]{2,0,1:T(4,128)}), f32[4,6,384]{2,0,1:T(4,128)S(1)}, u32[]{:S(2)}, u32[]{:S(2)}) async-start(f32[4,6,384]{2,0,1:T(4,128)} %copy.36), calls=%async_computation.2 | async-start | bytes 73728 | tf_op jit(solution)/shard_map/all_to_all | solution.py:121
Sparse Core Ops, SparseCore 0:
  13.1 41.2 all-gather.6
  190.8 52.8 reduce-scatter.1
